TPU v7x, 32 devices: a whole 2x2x4 slice. The times are simulated.
32 devices in a mesh: task: 4 (over x, core), param: 8 (over z, y).
Axes of the slice: x: 2, y: 2, z: 4, core: 2. Of those that a mesh axis runs over, the one named last changes fastest.
Arguments:
- acts: bfloat16 [128, 3584], replicated, may hold values from -6 to 6
- out_grads: bfloat16 [4, 128, 10240], P('task', None, 'param'), may hold values from -12 to 12
- order: int32 [4], replicated, may hold values from 0 to 3, each once
Outputs:
- update: float32 [3584, 10240], P('task', 'param')
- weights: float32 [4], replicated
All inputs are finite; a program needn't handle non-finite values.
Results may differ from a plain program's by a relative error of at most 0.0029.
Values may be sent and summed in bfloat16 or wider, within the bound.
A program may use at most 64 MiB of HBM per device.

v0:
```python
import jax
import jax.numpy as jnp
from jax import lax
from jax.sharding import PartitionSpec as P


def task_grads(acts_part, blocks):
    return jnp.einsum("td,ktc->kdc", acts_part, blocks, preferred_element_type=jnp.float32).astype(
        jnp.bfloat16
    )


def pcgrad_weights(gram, order):
    count = gram.shape[0]
    ids = jnp.arange(count, dtype=jnp.int32)

    def turn(step, mix):
        target = order[step]
        column = gram[:, target]
        onehot = (ids == target).astype(jnp.float32)
        dots = jnp.dot(mix, column, precision=lax.Precision.HIGHEST)
        scale = jnp.sum(column * onehot) + 1e-06
        change = jnp.minimum(dots, 0.0) / scale * (1.0 - onehot)
        return mix - change[:, None] * onehot[None, :]

    mix = lax.fori_loop(0, count, turn, jnp.eye(count, dtype=jnp.float32))
    return jnp.sum(mix, axis=0)


def shards(acts, out_grads, order):
    local = out_grads.shape[0]
    groups = lax.axis_size("task")
    group_id = lax.axis_index("task")
    total_tasks = local * groups
    part_rows = acts.shape[1] // groups
    acts_rows = lax.dynamic_slice_in_dim(acts, group_id * part_rows, part_rows, 1)
    everyone = lax.all_gather(out_grads, "task", axis=0, tiled=True)
    row_grads = task_grads(acts_rows, everyone)
    flat = row_grads.reshape(total_tasks, -1)
    partial_gram = jnp.dot(flat, flat.T, preferred_element_type=jnp.float32)
    gram = lax.psum(partial_gram, ("task", "param"))
    weights = pcgrad_weights(gram, order)
    combined = jnp.einsum(
        "k,ktc->tc", weights, everyone.astype(jnp.float32), precision=lax.Precision.HIGHEST
    ).astype(jnp.bfloat16)
    update = lax.dot_general(
        acts_rows, combined, (((0,), (0,)), ((), ())), preferred_element_type=jnp.float32
    )
    return (update, weights)


def solution(mesh):
    in_specs = (P(), P("task", None, "param"), P())
    out_specs = (P("task", "param"), P())
    return jax.shard_map(shards, mesh=mesh, in_specs=in_specs, out_specs=out_specs, check_vma=False)
```

profile of v0, /device:TPU:0, one launch (start us, length us, event | category | flops | bytes accessed | tf_op | source)
XLA Modules:
  0.0 130.1 jit_solution(3699769488526502229)
XLA Ops:
  7.2 0.0 copy-start
  7.2 0.0 all-gather.2.cloned.1.call-start
  7.2 0.7 all-gather.2.cloned.1.call-update
  7.9 22.5 %all-gather.2.cloned.1.call-done = bf16[4,128,1280]{2,1,0:T(8,128)(2,1)} async-done(((bf16[1,128,1280]{2,1,0:T(8,128)(2,1)}), bf16[4,128,1280]{2,1,0:T(8,128)(2,1)}) %all-gather.2.cloned.1.call-update) | async-done | bytes 1310736 | tf_op jit(solution)/shard_map/all_gather | solution.py:37
  30.5 0.0 copy-done
  30.5 3.9 %convolution_convert_fusion = bf16[896,4,1280]{2,0,1:T(8,128)(2,1)S(1)} fusion(bf16[4,128,1280]{2,1,0:T(8,128)(2,1)} %all-gather.2.cloned.1.call-done, bf16[128,3584]{1,0:T(8,128)(2,1)S(1)} %copy-done, s32[]{:T(128)S(6)} %select_n.15), kind=kOutput, calls=%fused_computation.10 | convolution fusion | flops 1178992640 | bytes 10715140 | tf_op jit(solution)/shard_map/td,ktc->kdc/dot_general | solution.py:8
  34.4 0.0 copy-start.3
  34.4 0.0 copy-start.1
  34.4 20.1 %fusion.9 = f32[4,4]{1,0:T(4,128)S(1)} fusion(bf16[896,4,1280]{2,0,1:T(8,128)(2,1)S(1)} %convolution_convert_fusion), kind=kOutput, calls=%fused_computation.15 | convolution fusion | flops 36700160 | bytes 9175104 | tf_op jit(solution)/shard_map/dot_general | solution.py:40
  54.4 39.3 %psum.7 = f32[4,4]{1,0:T(4,128)S(1)} all-reduce(f32[4,4]{1,0:T(4,128)S(1)} %fusion.9), channel_id=1, replica_groups=mesh['task'=4,'param'=8] {'task','param'}, use_global_device_ids=true, to_apply=%region_0.0 | all-reduce | flops 16 | bytes 128 | tf_op jit(solution)/shard_map/psum | solution.py:41
  93.7 0.1 copy.6
  93.8 0.0 copy-done.3
  93.8 23.9 %while.14 = (s32[]{:T(128)}, f32[4,4]{1,0:T(4,128)S(1)}, s32[4]{0:T(128)S(1)}, f32[4,4]{0,1:T(4,128)S(1)}, s32[]{:T(128)}, /*index=5*/s32[]{:T(128)}, s32[]{:T(128)}, f32[]{:T(128)}) while((s32[]{:T(128)}, f32[4,4]{1,0:T(4,128)S(1)}, s32[4]{0:T(128)S(1)}, f32[4,4]{0,1:T(4,128)S(1)}, s32[]{:T(128)}, /*index=5*/s32[]{:T(128)}, ...), condition=%wide.region_3.0_spmd.clone, body=%wide.region_1.0_spmd.clone.sunk | while | flops 273 | bytes 2939 | solution.py:26
  93.8 0.6 dynamic_slice.35
  96.4 1.3 fusion.24
  98.3 0.8 fusion.25
  99.1 0.7 compare_convert_fusion.2
  99.7 0.1 multiply_subtract_fusion.2
  99.8 0.6 dynamic_slice.35
  102.3 1.3 fusion.24
  104.3 0.8 fusion.25
  105.0 0.7 compare_convert_fusion.2
  105.7 0.1 multiply_subtract_fusion.2
  105.8 0.6 dynamic_slice.35
  108.3 1.3 fusion.24
  110.2 0.8 fusion.25
  111.0 0.7 compare_convert_fusion.2
  111.7 0.1 multiply_subtract_fusion.2
  111.7 0.6 dynamic_slice.35
  114.3 1.3 fusion.24
  116.2 0.8 fusion.25
  117.0 0.7 compare_convert_fusion.2
  117.6 0.1 multiply_subtract_fusion.2
  117.7 0.0 copy-done.1
  117.7 0.0 copy-start.2
  117.7 2.5 %fusion.7 = bf16[1,128,1280]{2,0,1:T(2,128)(2,1)S(1)} fusion(bf16[4,128,1280]{2,1,0:T(8,128)(2,1)S(1)} %copy-done.1, f32[4]{0:T(128)S(1)} %reduce_sum.22), kind=kOutput, calls=%fused_computation.13 | convolution fusion | flops 7864320 | bytes 1638416 | tf_op jit(solution)/shard_map/k,ktc->tc/dot_general | solution.py:43
  120.3 2.9 %fusion.10 = f32[896,1280]{1,0:T(8,128)} fusion(bf16[1,128,1280]{2,0,1:T(2,128)(2,1)S(1)} %fusion.7, bf16[128,3584]{1,0:T(8,128)(2,1)S(1)} %copy-done, s32[]{:T(128)S(6)} %select_n.15), kind=kOutput, calls=%fused_computation.17 | convolution fusion | flops 293601280 | bytes 5472260 | tf_op jit(solution)/shard_map/dot_general | solution.py:46
  123.2 0.0 copy-done.2
  (2 shorter events, 0.0 us)
Async XLA Ops:
  7.2 23.3 %copy-start = (bf16[128,3584]{1,0:T(8,128)(2,1)S(1)}, bf16[128,3584]{1,0:T(8,128)(2,1)}, u32[]{:S(2)}) copy-start(bf16[128,3584]{1,0:T(8,128)(2,1)} %param.5) | copy-start | bytes 2752516
  7.2 23.3 %all-gather.2.cloned.1.call-start = ((), (), s32[]{:S(2)}) async-start(), calls=%async_computation | async-start | bytes 1638400 | tf_op jit(solution)/shard_map/all_gather | solution.py:37
  34.4 59.5 %copy-start.3 = (s32[4]{0:T(128)S(1)}, s32[4]{0:T(128)}, u32[]{:S(2)}) copy-start(s32[4]{0:T(128)} %param.7) | copy-start | bytes 52
  34.4 83.4 %copy-start.1 = (bf16[4,128,1280]{2,1,0:T(8,128)(2,1)S(1)}, bf16[4,128,1280]{2,1,0:T(8,128)(2,1)}, u32[]{:S(2)}) copy-start(bf16[4,128,1280]{2,1,0:T(8,128)(2,1)} %all-gather.2.cloned.1.call-done) | copy-start | bytes 3932164
  117.7 5.5 %copy-start.2 = (f32[4]{0:T(128)}, f32[4]{0:T(128)S(1)}, u32[]{:S(2)}) copy-start(f32[4]{0:T(128)S(1)} %reduce_sum.22) | copy-start | bytes 52
Sparse Core Ops, SparseCore 0:
  9.5 20.8 all-gather.1
where the time goes:
time: 131 us; the launch traced here: 130 us
  blocking collectives  39.3 us (30%)
  matrix products  32.5 us (25%)
  waiting for transfers between devices  23.2 us (18%)
  between operations  14.1 us (11%)
  loops' own time  10.4 us (8%)
  other arithmetic  8.09 us (6%)
  local copies, waits for them, and re-layouts  2.45 us (2%)
    psum x1, blocking collectives, shards(): gram = lax.psum(partial_gram, ('task', 'param'))  39.3 us
    all_gather x1, waiting for transfers between devices, shards(): everyone = lax.all_gather(out_grads, 'task', axis=0, tiled=True)  22.5 us
    dot_general x1, matrix products, shards(): partial_gram = jnp.dot(flat, flat.T, preferred_element_type=jnp.float32)  20.1 us
    another operation x1, loops' own time, pcgrad_weights(): mix = lax.fori_loop(0, count, turn, jnp.eye(count, dtype=jnp.float32))  10.4 us
    reduce_sum x4, other arithmetic, turn(): scale = jnp.sum(column * onehot) + 1e-06  5.13 us
    dot_general x1, matrix products, task_grads(): jnp.einsum('td,ktc->kdc', acts_part, blocks, preferred_element_type=jnp.f...  3.88 us
    dot_general x4, matrix products, turn(): dots = jnp.dot(mix, column, precision=lax.Precision.HIGHEST)  3.12 us
    dot_general x1, matrix products, shards(): lax.dot_general(acts_rows, combined, (((0,), (0,)), ((), ())), preferred_...  2.94 us
  transfers between devices with their start and end apart: 1, of which 1 were waited for; matrix products, arithmetic and copies ran while one was open for 0% of the time, Pallas kernels for 0%

commit v1 on v0

v1 whole, which is shorter than its diff:
```python
import functools

import jax
import jax.numpy as jnp
from jax import lax
from jax.experimental import pallas as pl
from jax.experimental.pallas import tpu as pltpu
from jax.sharding import PartitionSpec as P

MESH = pl.DeviceIdType.MESH
LANES = 128


def task_device(index):
    return {"task": index}


def column_blocks(columns, groups):
    tiles = columns // LANES
    edges = [tiles * g // groups for g in range(groups + 1)]
    return [(edges[g] * LANES, (edges[g + 1] - edges[g]) * LANES) for g in range(groups)]


def pcgrad_weights(gram_row, order_ref, tasks):
    rows = max(8, tasks)
    sub = lax.broadcasted_iota(jnp.int32, (rows, LANES), 0)
    lane = lax.broadcasted_iota(jnp.int32, (rows, LANES), 1)
    flat = jnp.broadcast_to(gram_row, (rows, LANES))
    targets, columns, scales = [], [], []
    for step in range(tasks):
        target = order_ref[step]
        column = jnp.sum(jnp.where(lane == sub * tasks + target, flat, 0.0), axis=1, keepdims=True)
        scale = jnp.sum(jnp.where(lane == target * (tasks + 1), flat, 0.0), axis=1, keepdims=True)
        targets.append(target)
        columns.append(jnp.broadcast_to(column, (rows, LANES)))
        scales.append(scale[:1] + 1e-6)
    mix = jnp.where((sub == lane) & (sub < tasks), 1.0, 0.0)
    for target, column, scale in zip(targets, columns, scales):
        dots = jnp.sum(mix * column, axis=0, keepdims=True)
        change = jnp.minimum(dots, 0.0) / scale
        mix = mix - jnp.where((sub == target) & (lane != target), change, 0.0)
    return jnp.sum(mix, axis=1, keepdims=True)


def mixer(
    groups,
    others,
    order_ref,
    acts_hbm,
    grads_hbm,
    combined_ref,
    weights_ref,
    acts_v,
    every,
    kernel_mat,
    rows_ref,
    mine_ref,
    gath,
    local_sem,
    send_sem,
    near_recv,
    far_recv,
    fwd_send,
    fwd_recv,
    row_send,
    row_recv,
):
    me = lax.axis_index("task")
    place = lax.axis_index("param")
    core = lax.rem(me, 2)
    partner = me + 1 - 2 * core
    total = groups * others
    chips = groups // 2
    chip = me // 2
    linear = me * others + place
    tokens, columns = every.shape[1:]
    blocks = column_blocks(columns, groups)
    live = [index for index in range(groups) if blocks[index][1] > 0]

    load_grads = pltpu.make_async_copy(grads_hbm.at[0], every.at[me], local_sem.at[0])
    load_acts = pltpu.make_async_copy(acts_hbm, acts_v, local_sem.at[1])
    load_grads.start()
    load_acts.start()

    def device(index):
        return {"task": index // others, "param": lax.rem(index, others)}

    barrier = pltpu.get_barrier_semaphore()

    @pl.loop(1, total)
    def _(step):
        pl.semaphore_signal(
            barrier, inc=1, device_id=device(lax.rem(linear + step, total)), device_id_type=MESH
        )

    load_acts.wait()
    acts = acts_v[...]
    outer = lax.dot_general(acts, acts, (((1,), (1,)), ((), ())), preferred_element_type=jnp.float32)
    high = outer.astype(jnp.bfloat16)
    rest = outer - high.astype(jnp.float32)
    mid = rest.astype(jnp.bfloat16)
    low = (rest - mid.astype(jnp.float32)).astype(jnp.bfloat16)
    kernel_mat[0:tokens] = high
    kernel_mat[tokens : 2 * tokens] = mid
    kernel_mat[2 * tokens :] = low
    load_grads.wait()
    pl.semaphore_wait(barrier, total - 1)

    def block(task, index):
        start, size = blocks[index]
        return every.at[task, :, pl.ds(start, size)]

    def send(index, target, slot, recv):
        return pltpu.make_async_remote_copy(
            src_ref=block(me, index),
            dst_ref=block(me, index),
            send_sem=send_sem.at[slot, index],
            recv_sem=recv,
            device_id={"task": target},
            device_id_type=MESH,
        )

    across = pltpu.make_async_remote_copy(
        src_ref=every.at[me],
        dst_ref=every.at[me],
        send_sem=send_sem.at[0, 0],
        recv_sem=near_recv.at[me],
        device_id={"task": partner},
        device_id_type=MESH,
    )
    across.start()

    sends = []
    for hop in range(1, chips):
        for index in live:
            other = lax.rem(chip + hop, chips)
            target = other * 2 + index % 2
            first = other == index // 2

            @pl.when(first)
            def _():
                send(index, target, hop, near_recv.at[me]).start()

    for hop in range(1, chips):
        for index in live:
            other = lax.rem(chip + hop, chips)
            target = other * 2 + index % 2
            first = other == index // 2

            @pl.when(jnp.logical_not(first))
            def _():
                send(index, target, hop, far_recv.at[me, index]).start()

    def forward(task, index):
        return pltpu.make_async_remote_copy(
            src_ref=block(task, index),
            dst_ref=block(task, index),
            send_sem=fwd_send.at[task, index],
            recv_sem=fwd_recv.at[task, index],
            device_id={"task": partner},
            device_id_type=MESH,
        )

    def waiter(ref, sem):
        return pltpu.make_async_copy(ref, ref, sem)

    waiter(every.at[partner], near_recv.at[partner]).wait()
    for hop in range(1, chips):
        for source_core in range(2):
            task = lax.rem(chip + hop, chips) * 2 + source_core
            for index in live:

                @pl.when(me == index)
                def _():
                    waiter(block(task, index), near_recv.at[task]).wait()
                    forward(task, index).start()

    tiles = columns // LANES
    first_tile = (tiles * me) // groups
    count = (tiles * (me + 1)) // groups - first_tile
    sizes = [size // LANES for _, size in blocks]
    rows_ref[...] = jnp.zeros_like(rows_ref)
    pairs = [(i, j) for i in range(groups) for j in range(i, groups)]

    def share(slot):
        at = pl.multiple_of((first_tile + slot) * LANES, LANES)
        parts = [every[k, :, pl.ds(at, LANES)] for k in range(groups)]
        weighted = []
        for part in parts:
            wide = jnp.dot(kernel_mat[...], part, preferred_element_type=jnp.float32)
            weighted.append(wide[:tokens] + (wide[tokens : 2 * tokens] + wide[2 * tokens :]))
        plain = [part.astype(jnp.float32) for part in parts]
        for i, j in pairs:
            row = jnp.sum(weighted[i] * plain[j], axis=0, keepdims=True)
            spot = i * groups + j
            rows_ref[spot : spot + 1, :] += row
            if i != j:
                spot = j * groups + i
                rows_ref[spot : spot + 1, :] += row

    for slot in range(max(sizes)):
        if slot < min(sizes):
            share(slot)
        else:
            pl.when(count > slot)(functools.partial(share, slot))

    entries = groups * groups
    sums = jnp.sum(rows_ref[...], axis=1, keepdims=True)
    sub = lax.broadcasted_iota(jnp.int32, (entries, LANES), 0)
    lane = lax.broadcasted_iota(jnp.int32, (entries, LANES), 1)
    row = jnp.sum(jnp.where(sub == lane, sums, 0.0), axis=0, keepdims=True)
    mine_ref[...] = row
    gath[linear] = row

    @pl.loop(1, total)
    def _(step):
        pltpu.make_async_remote_copy(
            src_ref=mine_ref,
            dst_ref=gath.at[linear],
            send_sem=row_send,
            recv_sem=row_recv,
            device_id=device(lax.rem(linear + step, total)),
            device_id_type=MESH,
        ).start()

    for hop in range(1, chips):
        other = lax.rem(chip + hop, chips)
        for index in live:
            for source_core in range(2):
                task = other * 2 + source_core

                @pl.when((chip != index // 2) & (core == index % 2))
                def _():
                    waiter(block(task, index), far_recv.at[task, index]).wait()
                    forward(task, index).start()

    for hop in range(1, chips):
        other = lax.rem(chip + hop, chips)
        for index in live:
            for source_core in range(2):
                task = other * 2 + source_core

                @pl.when(core != index % 2)
                def _():
                    waiter(block(task, index), fwd_recv.at[task, index]).wait()

    bulk = gath.at[pl.ds(0, total - 1)]
    waiter(bulk, row_recv).wait()
    gram_row = jnp.sum(gath[...], axis=0)
    weights = pcgrad_weights(gram_row, order_ref, groups)

    @pl.loop(0, tiles)
    def _(tile):
        at = pl.ds(pl.multiple_of(tile * LANES, LANES), LANES)
        mixed = weights[0:1] * every[0, :, at].astype(jnp.float32)
        for k in range(1, groups):
            mixed = mixed + weights[k : k + 1] * every[k, :, at].astype(jnp.float32)
        combined_ref[:, at] = mixed.astype(jnp.bfloat16)

    weights_ref[...] = jnp.broadcast_to(weights, weights_ref.shape)

    waiter(bulk, row_send).wait()
    waiter(every.at[me], send_sem.at[0, 0]).wait()
    for hop in range(1, chips):
        other = lax.rem(chip + hop, chips)
        for index in live:
            waiter(block(me, index), send_sem.at[hop, index]).wait()
            for source_core in range(2):
                task = other * 2 + source_core

                @pl.when(core == index % 2)
                def _():
                    waiter(block(task, index), fwd_send.at[task, index]).wait()


def shards(acts, out_grads, order):
    groups = lax.axis_size("task")
    others = lax.axis_size("param")
    total = groups * others
    tokens, columns = out_grads.shape[1:]
    part_rows = acts.shape[1] // groups
    dma = pltpu.SemaphoreType.DMA
    combined, weights = pl.pallas_call(
        functools.partial(mixer, groups, others),
        out_shape=(
            jax.ShapeDtypeStruct((tokens, columns), jnp.bfloat16),
            jax.ShapeDtypeStruct((max(8, groups), LANES), jnp.float32),
        ),
        in_specs=[
            pl.BlockSpec(memory_space=pltpu.SMEM),
            pl.BlockSpec(memory_space=pl.ANY),
            pl.BlockSpec(memory_space=pl.ANY),
        ],
        out_specs=(
            pl.BlockSpec(memory_space=pltpu.VMEM),
            pl.BlockSpec(memory_space=pltpu.VMEM),
        ),
        scratch_shapes=[
            pltpu.VMEM(acts.shape, jnp.bfloat16),
            pltpu.VMEM((groups, tokens, columns), jnp.bfloat16),
            pltpu.VMEM((3 * tokens, tokens), jnp.bfloat16),
            pltpu.VMEM((groups * groups, LANES), jnp.float32),
            pltpu.VMEM((1, LANES), jnp.float32),
            pltpu.VMEM((total, 1, LANES), jnp.float32),
            dma((2,)),
            dma((groups, groups)),
            dma((groups,)),
            dma((groups, groups)),
            dma((groups, groups)),
            dma((groups, groups)),
            dma,
            dma,
        ],
        compiler_params=pltpu.CompilerParams(collective_id=0, has_side_effects=True),
        name="mixer",
    )(order, acts, out_grads)
    group_id = lax.axis_index("task")
    acts_rows = lax.dynamic_slice_in_dim(acts, group_id * part_rows, part_rows, 1)
    update = lax.dot_general(
        acts_rows, combined, (((0,), (0,)), ((), ())), preferred_element_type=jnp.float32
    )
    return (update, weights[:groups, 0])


def solution(mesh):
    in_specs = (P(), P("task", None, "param"), P())
    out_specs = (P("task", "param"), P())
    return jax.shard_map(shards, mesh=mesh, in_specs=in_specs, out_specs=out_specs, check_vma=False)
```

time: 131 us -> 25.8 us (0.20)
  blocking collectives: 39.3 us -> 0 us
  matrix products: 32.5 us -> 4.03 us
  waiting for transfers between devices: 23.2 us -> 0 us
  Pallas kernels: 0 us -> 19.6 us
  between operations: 14.1 us -> 0.64 us
  loops' own time: 10.4 us -> 0 us
  other arithmetic: 8.09 us -> 0 us
    psum x1 -> x0, blocking collectives: 39.3 us -> none  [shards(): gram = lax.psum(partial_gram, ('task', 'param'))]
    dot_general x7 -> x0, matrix products: 29.6 us -> none  [the longest x1 20.1 us: shards(): partial_gram = jnp.dot(flat, flat.T, preferred_element_type=jnp.float32)]
    all_gather x1 -> x0, waiting for transfers between devices: 22.5 us -> none  [shards(): everyone = lax.all_gather(out_grads, 'task', axis=0, tiled=True)]
    pallas_call x0 -> x1, Pallas kernels: none -> 19.6 us  [shards(): pl.pallas_call(functools.partial(mixer, groups, others), out_shape=(jax.S...]
    another operation x1 -> x0, loops' own time: 10.4 us -> none  [pcgrad_weights(): mix = lax.fori_loop(0, count, turn, jnp.eye(count, dtype=jnp.float32))]
    reduce_sum x5 -> x0, other arithmetic: 5.15 us -> none  [the longest x4 5.13 us: turn(): scale = jnp.sum(column * onehot) + 1e-06]
    convert_element_type x5 -> x0, other arithmetic: 2.63 us -> none  [the longest x4 2.63 us: turn(): onehot = (ids == target).astype(jnp.float32)]
    dynamic_slice x4 -> x0, local copies, waits for them, and re-layouts: 2.33 us -> none  [turn(): target = order[step]]
  transfers between devices with their start and end apart: 1 -> 0, of which waited for: 1 -> 0; matrix products, arithmetic and copies ran while one was open for 0% -> 0% of each run, Pallas kernels for 0% -> 0%
where the time goes in v1:
time: 25.8 us; the launch traced here: 25.6 us
  Pallas kernels  19.6 us (76%)
  matrix products  4.03 us (16%)
  local copies, waits for them, and re-layouts  1.31 us (5%)
  between operations  0.64 us (2%)
    pallas_call x1, Pallas kernels, shards(): pl.pallas_call(functools.partial(mixer, groups, others), out_shape=(jax.S...  19.6 us
    dot_general x1, matrix products, shards(): lax.dot_general(acts_rows, combined, (((0,), (0,)), ((), ())), preferred_...  4.03 us
    slice x1, local copies, waits for them, and re-layouts, shards(): return (update, weights[:groups, 0])  1.31 us

profile of v1, /device:TPU:0, one launch (start us, length us, event | category | flops | bytes accessed | tf_op | source)
XLA Modules:
  0.0 25.6 jit_solution(9282601313998315914)
XLA Ops:
  0.6 19.6 %mixer.1 = (bf16[128,1280]{1,0:T(8,128)(2,1)}, f32[8,128]{1,0:T(8,128)}) custom-call(s32[4]{0:T(128)} %order_ref.1, bf16[128,3584]{1,0:T(8,128)(2,1)} %acts_hbm.1, bf16[1,128,1280]{2,1,0:T(8,128)(2,1)} %grads_hbm.1), custom_call_target="tpu_custom_call" | custom-call | tf_op jit(solution)/shard_map/mixer/pallas_call | solution.py:283
  20.2 1.3 %slice_reduce_fusion = f32[4]{0:T(128)} fusion(f32[8,128]{1,0:T(8,128)} %get-tuple-element.5), kind=kLoop, calls=%fused_computation.2 | loop fusion | bytes 32 | tf_op jit(solution)/shard_map/slice | solution.py:322
  21.5 4.0 %fusion = f32[896,1280]{1,0:T(8,128)} fusion(bf16[128,1280]{1,0:T(8,128)(2,1)} %get-tuple-element.4, bf16[128,3584]{1,0:T(8,128)(2,1)} %acts_hbm.1, s32[]{:T(128)S(6)} %select_n.3), kind=kOutput, calls=%fused_computation | convolution fusion | flops 293601280 | bytes 5144580 | tf_op jit(solution)/shard_map/dot_general | solution.py:319

commit v2 on v1

v2 whole, which is shorter than its diff:
```python
import functools

import jax
import jax.numpy as jnp
from jax import lax
from jax.experimental import pallas as pl
from jax.experimental.pallas import tpu as pltpu
from jax.sharding import PartitionSpec as P

MESH = pl.DeviceIdType.MESH
LANES = 128
VMEM_BYTES = 67043328


def column_blocks(columns, groups):
    tiles = columns // LANES
    edges = [tiles * g // groups for g in range(groups + 1)]
    return [(edges[g] * LANES, (edges[g + 1] - edges[g]) * LANES) for g in range(groups)]


def pcgrad_weights(gram_row, order_ref, tasks):
    rows = max(8, tasks)
    sub = lax.broadcasted_iota(jnp.int32, (rows, LANES), 0)
    lane = lax.broadcasted_iota(jnp.int32, (rows, LANES), 1)
    flat = jnp.broadcast_to(gram_row, (rows, LANES))
    targets, columns, scales = [], [], []
    for step in range(tasks):
        target = order_ref[step]
        column = jnp.sum(jnp.where(lane == sub * tasks + target, flat, 0.0), axis=1, keepdims=True)
        scale = jnp.sum(jnp.where(lane == target * (tasks + 1), flat, 0.0), axis=1, keepdims=True)
        targets.append(target)
        columns.append(jnp.broadcast_to(column, (rows, LANES)))
        scales.append(scale[:1] + 1e-6)
    mix = jnp.where((sub == lane) & (sub < tasks), 1.0, 0.0)
    for target, column, scale in zip(targets, columns, scales):
        dots = jnp.sum(mix * column, axis=0, keepdims=True)
        change = jnp.minimum(dots, 0.0) / scale
        mix = mix - jnp.where((sub == target) & (lane != target), change, 0.0)
    return jnp.sum(mix, axis=1, keepdims=True)


def mixer(
    groups,
    others,
    order_ref,
    acts_hbm,
    grads_hbm,
    combined_ref,
    acts_t,
    weights_ref,
    acts_v,
    every,
    kernel_mat,
    own_prod,
    partner_prod,
    rows_ref,
    turned,
    mine_ref,
    gath,
    local_sem,
    send_sem,
    near_recv,
    far_recv,
    fwd_send,
    fwd_recv,
    row_send,
    row_recv,
):
    me = lax.axis_index("task")
    place = lax.axis_index("param")
    core = lax.rem(me, 2)
    partner = me + 1 - 2 * core
    total = groups * others
    chips = groups // 2
    chip = me // 2
    linear = me * others + place
    tokens, columns = every.shape[1:]
    blocks = column_blocks(columns, groups)
    live = [index for index in range(groups) if blocks[index][1] > 0]

    load_grads = pltpu.make_async_copy(grads_hbm.at[0], every.at[me], local_sem.at[0])
    load_acts = pltpu.make_async_copy(acts_hbm, acts_v, local_sem.at[1])
    load_grads.start()
    load_acts.start()

    def device(index):
        return {"task": index // others, "param": lax.rem(index, others)}

    barrier = pltpu.get_barrier_semaphore()

    @pl.loop(1, total)
    def _(step):
        pl.semaphore_signal(
            barrier, inc=1, device_id=device(lax.rem(linear + step, total)), device_id_type=MESH
        )

    load_grads.wait()
    pl.semaphore_wait(barrier, total - 1)

    def block(task, index):
        start, size = blocks[index]
        return every.at[task, :, pl.ds(start, size)]

    def send(index, target, slot, recv):
        return pltpu.make_async_remote_copy(
            src_ref=block(me, index),
            dst_ref=block(me, index),
            send_sem=send_sem.at[slot, index],
            recv_sem=recv,
            device_id={"task": target},
            device_id_type=MESH,
        )

    across = pltpu.make_async_remote_copy(
        src_ref=every.at[me],
        dst_ref=every.at[me],
        send_sem=send_sem.at[0, 0],
        recv_sem=near_recv.at[me],
        device_id={"task": partner},
        device_id_type=MESH,
    )
    across.start()

    for hop in range(1, chips):
        for index in live:
            other = lax.rem(chip + hop, chips)
            target = other * 2 + index % 2
            first = other == index // 2

            @pl.when(first)
            def _():
                send(index, target, hop, near_recv.at[me]).start()

    for hop in range(1, chips):
        for index in live:
            other = lax.rem(chip + hop, chips)
            target = other * 2 + index % 2
            first = other == index // 2

            @pl.when(jnp.logical_not(first))
            def _():
                send(index, target, hop, far_recv.at[me, index]).start()

    def forward(task, index):
        return pltpu.make_async_remote_copy(
            src_ref=block(task, index),
            dst_ref=block(task, index),
            send_sem=fwd_send.at[task, index],
            recv_sem=fwd_recv.at[task, index],
            device_id={"task": partner},
            device_id_type=MESH,
        )

    def waiter(ref, sem):
        return pltpu.make_async_copy(ref, ref, sem)

    load_acts.wait()
    acts = acts_v[...]
    outer = lax.dot_general(acts, acts, (((1,), (1,)), ((), ())), preferred_element_type=jnp.float32)
    high = outer.astype(jnp.bfloat16)
    rest = outer - high.astype(jnp.float32)
    mid = rest.astype(jnp.bfloat16)
    low = (rest - mid.astype(jnp.float32)).astype(jnp.bfloat16)
    kernel_mat[0:tokens] = high
    kernel_mat[tokens : 2 * tokens] = mid
    kernel_mat[2 * tokens :] = low

    def weigh(part):
        wide = jnp.dot(kernel_mat[...], part, preferred_element_type=jnp.float32)
        return wide[:tokens] + (wide[tokens : 2 * tokens] + wide[2 * tokens :])

    def fold(product):
        while product.shape[1] > LANES:
            half = product.shape[1] // 2
            product = product[:, :half] + product[:, half:]
        return jnp.sum(product.reshape(tokens // 8, 8, LANES), axis=0)

    rows_ref[...] = jnp.zeros_like(rows_ref)
    width = 2 * LANES if columns % (2 * LANES) == 0 else LANES
    for start in range(0, columns, width):
        part = every[me, :, start : start + width]
        prod = weigh(part)
        own_prod[:, start : start + width] = prod
        rows_ref[0] += fold(prod * part.astype(jnp.float32))
    waiter(every.at[partner], near_recv.at[partner]).wait()
    for start in range(0, columns, width):
        part = every[partner, :, start : start + width].astype(jnp.float32)
        rows_ref[1] += fold(own_prod[:, start : start + width] * part)

    tiles = columns // LANES
    first_tile = (tiles * me) // groups
    count = (tiles * (me + 1)) // groups - first_tile
    sizes = [size // LANES for _, size in blocks]

    def at(slot):
        return pl.ds(pl.multiple_of((first_tile + slot) * LANES, LANES), LANES)

    def over_share(body):
        for slot in range(max(sizes)):
            if slot < min(sizes):
                body(slot)
            else:
                pl.when(count > slot)(functools.partial(body, slot))

    def weigh_partner(slot):
        partner_prod[slot] = weigh(every[partner, :, at(slot)])

    over_share(weigh_partner)

    distant = []
    for hop in range(1, chips):
        for source_core in range(2):
            task = lax.rem(chip + hop, chips) * 2 + source_core
            distant.append((hop, task))
            for index in live:

                @pl.when(me == index)
                def _():
                    waiter(block(task, index), near_recv.at[task]).wait()
                    forward(task, index).start()

    pairs = [(me, me), (me, partner)]
    for _, task in distant:
        pairs += [(me, task), (partner, task)]
    for n, (hop, task) in enumerate(distant):
        pairs += [(task, late) for later, late in distant[n + 1 :] if later != hop]

    def cross(slot):
        parts = [every[task, :, at(slot)] for _, task in distant]
        wide = [part.astype(jnp.float32) for part in parts]
        own, near = own_prod[:, at(slot)], partner_prod[slot]
        spot = 2
        for part in wide:
            rows_ref[spot] += fold(own * part)
            rows_ref[spot + 1] += fold(near * part)
            spot += 2
        for n, (hop, _) in enumerate(distant):
            if any(later != hop for later, _ in distant[n + 1 :]):
                prod = weigh(parts[n])
                for k in range(n + 1, len(distant)):
                    if distant[k][0] != hop:
                        rows_ref[spot] += fold(prod * wide[k])
                        spot += 1

    over_share(cross)
    sums = jnp.sum(jnp.sum(rows_ref[...], axis=1), axis=1, keepdims=True)
    lane = lax.broadcasted_iota(jnp.int32, (1, LANES), 1)
    row = jnp.zeros((1, LANES), jnp.float32)
    for spot, (i, j) in enumerate(pairs):
        entry = sums[spot : spot + 1]
        if spot == 1:
            entry = 0.5 * entry
        row += jnp.where((lane == i * groups + j) | (lane == j * groups + i), entry, 0.0)
    mine_ref[...] = row
    gath[linear] = row

    @pl.loop(1, total)
    def _(step):
        pltpu.make_async_remote_copy(
            src_ref=mine_ref,
            dst_ref=gath.at[linear],
            send_sem=row_send,
            recv_sem=row_recv,
            device_id=device(lax.rem(linear + step, total)),
            device_id_type=MESH,
        ).start()

    for hop in range(1, chips):
        other = lax.rem(chip + hop, chips)
        for index in live:
            for source_core in range(2):
                task = other * 2 + source_core

                @pl.when((chip != index // 2) & (core == index % 2))
                def _():
                    waiter(block(task, index), far_recv.at[task, index]).wait()
                    forward(task, index).start()

    for hop in range(1, chips):
        other = lax.rem(chip + hop, chips)
        for index in live:
            for source_core in range(2):
                task = other * 2 + source_core

                @pl.when(core != index % 2)
                def _():
                    waiter(block(task, index), fwd_recv.at[task, index]).wait()

    part_rows = acts_t.shape[0]
    if part_rows % LANES == 0:
        for start in range(0, part_rows, LANES):
            source = pl.ds(pl.multiple_of(me * part_rows + start, LANES), LANES)
            acts_t[start : start + LANES, :] = acts_v[:, source].T
    else:
        for start in range(0, acts_v.shape[1], LANES):
            turned[start : start + LANES, :] = acts_v[:, start : start + LANES].T
        acts_t[...] = turned[pl.ds(pl.multiple_of(me * part_rows, 16), part_rows), :]

    bulk = gath.at[pl.ds(0, total - 1)]
    waiter(bulk, row_recv).wait()
    gram_row = jnp.sum(gath[...], axis=0)
    weights = pcgrad_weights(gram_row, order_ref, groups)

    @pl.loop(0, tiles)
    def _(tile):
        at = pl.ds(pl.multiple_of(tile * LANES, LANES), LANES)
        mixed = weights[0:1] * every[0, :, at].astype(jnp.float32)
        for k in range(1, groups):
            mixed = mixed + weights[k : k + 1] * every[k, :, at].astype(jnp.float32)
        combined_ref[:, at] = mixed.astype(jnp.bfloat16)

    diagonal = lax.broadcasted_iota(jnp.int32, (weights.shape[0], LANES), 0) == (
        lax.broadcasted_iota(jnp.int32, (weights.shape[0], LANES), 1)
    )
    weights_ref[...] = jnp.sum(jnp.where(diagonal, weights, 0.0), axis=0, keepdims=True)

    waiter(bulk, row_send).wait()
    waiter(every.at[me], send_sem.at[0, 0]).wait()
    for hop in range(1, chips):
        other = lax.rem(chip + hop, chips)
        for index in live:
            waiter(block(me, index), send_sem.at[hop, index]).wait()
            for source_core in range(2):
                task = other * 2 + source_core

                @pl.when(core == index % 2)
                def _():
                    waiter(block(task, index), fwd_send.at[task, index]).wait()


def expand(acts_t, combined, weights_row, update_hbm, weights_ref, buffer, sems):
    rows = acts_t.shape[0]
    step = LANES if rows % LANES == 0 else rows
    copies = []
    for n, start in enumerate(range(0, rows, step)):
        span = pl.ds(start, step)
        buffer[span, :] = jnp.dot(
            acts_t[span, :], combined[...], preferred_element_type=jnp.float32
        )
        copy = pltpu.make_async_copy(buffer.at[span], update_hbm.at[span], sems.at[n])
        copy.start()
        copies.append(copy)
    weights_ref[...] = weights_row[0, : weights_ref.shape[0]]
    for copy in copies:
        copy.wait()


def shards(acts, out_grads, order):
    groups = lax.axis_size("task")
    others = lax.axis_size("param")
    total = groups * others
    tokens, columns = out_grads.shape[1:]
    model = acts.shape[1]
    part_rows = model // groups
    most = max(size for _, size in column_blocks(columns, groups)) // LANES
    remote = groups - 2
    pair_count = 2 + 2 * remote + remote * (remote - 2) // 2
    aligned = part_rows % LANES == 0
    kept = 2 * tokens * (columns + part_rows) + 2**16
    dma = pltpu.SemaphoreType.DMA
    vmem = pl.BlockSpec(memory_space=pltpu.VMEM)
    combined, acts_t, weights_row = pl.pallas_call(
        functools.partial(mixer, groups, others),
        out_shape=(
            pltpu.VMEM((tokens, columns), jnp.bfloat16),
            pltpu.VMEM((part_rows, tokens), jnp.bfloat16),
            pltpu.VMEM((1, LANES), jnp.float32),
        ),
        in_specs=[
            pl.BlockSpec(memory_space=pltpu.SMEM),
            pl.BlockSpec(memory_space=pltpu.HBM),
            pl.BlockSpec(memory_space=pltpu.HBM),
        ],
        out_specs=(vmem, vmem, vmem),
        scratch_shapes=[
            pltpu.VMEM(acts.shape, jnp.bfloat16),
            pltpu.VMEM((groups, tokens, columns), jnp.bfloat16),
            pltpu.VMEM((3 * tokens, tokens), jnp.bfloat16),
            pltpu.VMEM((tokens, columns), jnp.float32),
            pltpu.VMEM((most, tokens, LANES), jnp.float32),
            pltpu.VMEM((pair_count, 8, LANES), jnp.float32),
            pltpu.VMEM((16 if aligned else model, tokens), jnp.bfloat16),
            pltpu.VMEM((1, LANES), jnp.float32),
            pltpu.VMEM((total, 1, LANES), jnp.float32),
            dma((2,)),
            dma((groups, groups)),
            dma((groups,)),
            dma((groups, groups)),
            dma((groups, groups)),
            dma((groups, groups)),
            dma,
            dma,
        ],
        compiler_params=pltpu.CompilerParams(
            collective_id=0, has_side_effects=True, vmem_limit_bytes=VMEM_BYTES - kept
        ),
        name="mixer",
    )(order, acts, out_grads)
    update, weights = pl.pallas_call(
        expand,
        out_shape=(
            jax.ShapeDtypeStruct((part_rows, columns), jnp.float32),
            jax.ShapeDtypeStruct((groups,), jnp.float32),
        ),
        in_specs=[vmem, vmem, vmem],
        out_specs=(pl.BlockSpec(memory_space=pl.ANY), vmem),
        scratch_shapes=[
            pltpu.VMEM((part_rows, columns), jnp.float32),
            dma((pl.cdiv(part_rows, LANES),)),
        ],
        compiler_params=pltpu.CompilerParams(vmem_limit_bytes=24 * 2**20),
        name="expand",
    )(acts_t, combined, weights_row)
    return (update, weights)


def solution(mesh):
    in_specs = (P(), P("task", None, "param"), P())
    out_specs = (P("task", "param"), P())
    return jax.shard_map(shards, mesh=mesh, in_specs=in_specs, out_specs=out_specs, check_vma=False)
```

time: 25.8 us -> 22.8 us (0.88)
  matrix products: 4.03 us -> 0 us
  Pallas kernels: 19.6 us -> 22 us
  local copies, waits for them, and re-layouts: 1.31 us -> 0 us
    dot_general x1 -> x0, matrix products: 4.03 us -> none  [shards(): lax.dot_general(acts_rows, combined, (((0,), (0,)), ((), ())), preferred_...]
    pallas_call x1 -> x2, Pallas kernels: 19.6 us -> 22 us  [the longest x1 19.1 us: shards(): pl.pallas_call(functools.partial(mixer, groups, others), out_shape=(pltpu...]
    slice x1 -> x0, local copies, waits for them, and re-layouts: 1.31 us -> none  [shards(): return (update, weights[:groups, 0])]
where the time goes in v2:
time: 22.8 us; the launch traced here: 22.7 us
  Pallas kernels  22 us (96%)
  between operations  0.64 us (3%)
    pallas_call x1, Pallas kernels, shards(): pl.pallas_call(functools.partial(mixer, groups, others), out_shape=(pltpu...  19.1 us
    pallas_call x1, Pallas kernels, shards(): pl.pallas_call(expand, out_shape=(jax.ShapeDtypeStruct((part_rows, column...  2.94 us

profile of v2, /device:TPU:0, one launch (start us, length us, event | category | flops | bytes accessed | tf_op | source)
XLA Modules:
  0.0 22.7 jit_solution(15657927227292346868)
XLA Ops:
  0.6 19.1 %mixer.1 = (bf16[128,1280]{1,0:T(8,128)(2,1)S(1)}, bf16[896,128]{1,0:T(8,128)(2,1)S(1)}, f32[1,128]{1,0:T(1,128)S(1)}) custom-call(s32[4]{0:T(128)} %order_ref.1, bf16[128,3584]{1,0:T(8,128)(2,1)} %acts_hbm.1, bf16[1,128,1280]{2,1,0:T(8,128)(2,1)} %grads_hbm.1), custom_call_target="tpu_custom_call" | custom-call | tf_op jit(solution)/shard_map/mixer/pallas_call | solution.py:362
  19.7 2.9 %expand.1 = (f32[896,1280]{1,0:T(8,128)}, f32[4]{0:T(128)}) custom-call(bf16[896,128]{1,0:T(8,128)(2,1)S(1)} %get-tuple-element.5.acts_t, bf16[128,1280]{1,0:T(8,128)(2,1)S(1)} %get-tuple-element.6.combined, f32[1,128]{1,0:T(1,128)S(1)} %get-tuple-element.7.weights_row), custom_call_target="tpu_custom_call" | custom-call | tf_op jit(solution)/shard_map/expand/pallas_call | solution.py:399

commit v3 on v2

--- a/solution.py
+++ b/solution.py
@@ -65,6 +65,7 @@
     fwd_recv,
     row_send,
     row_recv,
+    round_sem,
 ):
     me = lax.axis_index("task")
     place = lax.axis_index("param")
@@ -83,19 +84,41 @@
     load_grads.start()
     load_acts.start()
 
-    def device(index):
-        return {"task": index // others, "param": lax.rem(index, others)}
+    bits = (others - 1).bit_length()
+    doubling = others == 1 << bits
+
+    def flipped(mask):
+        index = place
+        for bit in range(bits):
+            if mask >> bit & 1:
+                index = index + (1 << bit) * (1 - 2 * lax.rem(place // (1 << bit), 2))
+        return index
+
+    def signal(semaphore, device):
+        pl.semaphore_signal(semaphore, inc=1, device_id=device, device_id_type=MESH)
+
+    tasks_from_me = [lax.rem(me + step, groups) for step in range(groups)]
+    if doubling:
+        places_from_me = [flipped(mask) for mask in range(others)]
+    else:
+        places_from_me = [lax.rem(place + step, others) for step in range(others)]
+    peers = [
+        {"task": task, "param": spot}
+        for far, spot in reversed(list(enumerate(places_from_me)))
+        for step, task in reversed(list(enumerate(tasks_from_me)))
+        if far or step
+    ]
 
     barrier = pltpu.get_barrier_semaphore()
-
-    @pl.loop(1, total)
-    def _(step):
-        pl.semaphore_signal(
-            barrier, inc=1, device_id=device(lax.rem(linear + step, total)), device_id_type=MESH
-        )
-
+    if doubling:
+        greeted = [{"task": task} for task in tasks_from_me[1:]]
+        greeted += [{"param": flipped(1 << bit)} for bit in range(bits)]
+    else:
+        greeted = peers
+    for device in greeted:
+        signal(barrier, device)
     load_grads.wait()
-    pl.semaphore_wait(barrier, total - 1)
+    pl.semaphore_wait(barrier, len(greeted))
 
     def block(task, index):
         start, size = blocks[index]
@@ -154,6 +177,15 @@
     def waiter(ref, sem):
         return pltpu.make_async_copy(ref, ref, sem)
 
+    def spread(bit):
+        if doubling and bit < bits:
+            signal(round_sem.at[bit], {"param": flipped(1 << bit)})
+
+    def learn(bit):
+        if doubling and bit < bits:
+            pl.semaphore_wait(round_sem.at[bit], 1)
+
+    spread(0)
     load_acts.wait()
     acts = acts_v[...]
     outer = lax.dot_general(acts, acts, (((1,), (1,)), ((), ())), preferred_element_type=jnp.float32)
@@ -206,6 +238,10 @@
         partner_prod[slot] = weigh(every[partner, :, at(slot)])
 
     over_share(weigh_partner)
+    for bit in range(bits):
+        if bit > 0:
+            spread(bit)
+        learn(bit)
 
     distant = []
     for hop in range(1, chips):
@@ -254,14 +290,13 @@
     mine_ref[...] = row
     gath[linear] = row
 
-    @pl.loop(1, total)
-    def _(step):
+    for device in peers:
         pltpu.make_async_remote_copy(
             src_ref=mine_ref,
             dst_ref=gath.at[linear],
             send_sem=row_send,
             recv_sem=row_recv,
-            device_id=device(lax.rem(linear + step, total)),
+            device_id=device,
             device_id_type=MESH,
         ).start()
 
@@ -390,6 +425,7 @@
             dma((groups, groups)),
             dma,
             dma,
+            pltpu.SemaphoreType.REGULAR((max(1, (others - 1).bit_length()),)),
         ],
         compiler_params=pltpu.CompilerParams(
             collective_id=0, has_side_effects=True, vmem_limit_bytes=VMEM_BYTES - kept

time: 22.8 us -> 20.9 us (0.917)
  Pallas kernels: 22 us -> 20.1 us
    pallas_call x1, Pallas kernels: 19.1 us -> 17.2 us  [shards(): pl.pallas_call(functools.partial(mixer, groups, others), out_shape=(pltpu...]
where the time goes in v3:
time: 20.9 us; the launch traced here: 20.7 us
  Pallas kernels  20.1 us (96%)
  between operations  0.64 us (3%)
    pallas_call x1, Pallas kernels, shards(): pl.pallas_call(functools.partial(mixer, groups, others), out_shape=(pltpu...  17.2 us
    pallas_call x1, Pallas kernels, shards(): pl.pallas_call(expand, out_shape=(jax.ShapeDtypeStruct((part_rows, column...  2.94 us

profile of v3, /device:TPU:0, one launch (start us, length us, event | category | flops | bytes accessed | tf_op | source)
XLA Modules:
  0.0 20.7 jit_solution(2033805633593854806)
XLA Ops:
  0.6 17.2 %mixer.1 = (bf16[128,1280]{1,0:T(8,128)(2,1)S(1)}, bf16[896,128]{1,0:T(8,128)(2,1)S(1)}, f32[1,128]{1,0:T(1,128)S(1)}) custom-call(s32[4]{0:T(128)} %order_ref.1, bf16[128,3584]{1,0:T(8,128)(2,1)} %acts_hbm.1, bf16[1,128,1280]{2,1,0:T(8,128)(2,1)} %grads_hbm.1), custom_call_target="tpu_custom_call" | custom-call | tf_op jit(solution)/shard_map/mixer/pallas_call | solution.py:397
  17.8 2.9 %expand.1 = (f32[896,1280]{1,0:T(8,128)}, f32[4]{0:T(128)}) custom-call(bf16[896,128]{1,0:T(8,128)(2,1)S(1)} %get-tuple-element.5.acts_t, bf16[128,1280]{1,0:T(8,128)(2,1)S(1)} %get-tuple-element.6.combined, f32[1,128]{1,0:T(1,128)S(1)} %get-tuple-element.7.weights_row), custom_call_target="tpu_custom_call" | custom-call | tf_op jit(solution)/shard_map/expand/pallas_call | solution.py:435

commit v4 on v3

--- a/solution.py
+++ b/solution.py
@@ -30,11 +30,11 @@
         scale = jnp.sum(jnp.where(lane == target * (tasks + 1), flat, 0.0), axis=1, keepdims=True)
         targets.append(target)
         columns.append(jnp.broadcast_to(column, (rows, LANES)))
-        scales.append(scale[:1] + 1e-6)
+        scales.append(1.0 / (scale[:1] + 1e-6))
     mix = jnp.where((sub == lane) & (sub < tasks), 1.0, 0.0)
     for target, column, scale in zip(targets, columns, scales):
         dots = jnp.sum(mix * column, axis=0, keepdims=True)
-        change = jnp.minimum(dots, 0.0) / scale
+        change = jnp.minimum(dots, 0.0) * scale
         mix = mix - jnp.where((sub == target) & (lane != target), change, 0.0)
     return jnp.sum(mix, axis=1, keepdims=True)
 
@@ -42,7 +42,7 @@
 def mixer(
     groups,
     others,
-    order_ref,
+    order_hbm,
     acts_hbm,
     grads_hbm,
     combined_ref,
@@ -66,6 +66,7 @@
     row_send,
     row_recv,
     round_sem,
+    order_ref,
 ):
     me = lax.axis_index("task")
     place = lax.axis_index("param")
@@ -83,6 +84,8 @@
     load_acts = pltpu.make_async_copy(acts_hbm, acts_v, local_sem.at[1])
     load_grads.start()
     load_acts.start()
+    load_order = pltpu.make_async_copy(order_hbm, order_ref, local_sem.at[2])
+    load_order.start()
 
     bits = (others - 1).bit_length()
     doubling = others == 1 << bits
@@ -154,15 +157,18 @@
             def _():
                 send(index, target, hop, near_recv.at[me]).start()
 
-    for hop in range(1, chips):
-        for index in live:
-            other = lax.rem(chip + hop, chips)
-            target = other * 2 + index % 2
-            first = other == index // 2
-
-            @pl.when(jnp.logical_not(first))
-            def _():
-                send(index, target, hop, far_recv.at[me, index]).start()
+    def send_rest(parity):
+        for hop in range(1, chips):
+            for index in live:
+                if index % 2 == parity:
+                    other = lax.rem(chip + hop, chips)
+                    target = other * 2 + index % 2
+
+                    @pl.when(other != index // 2)
+                    def _():
+                        send(index, target, hop, far_recv.at[me, index]).start()
+
+    send_rest(1)
 
     def forward(task, index):
         return pltpu.make_async_remote_copy(
@@ -300,6 +306,8 @@
             device_id_type=MESH,
         ).start()
 
+    send_rest(0)
+
     for hop in range(1, chips):
         other = lax.rem(chip + hop, chips)
         for index in live:
@@ -331,12 +339,13 @@
             turned[start : start + LANES, :] = acts_v[:, start : start + LANES].T
         acts_t[...] = turned[pl.ds(pl.multiple_of(me * part_rows, 16), part_rows), :]
 
+    load_order.wait()
     bulk = gath.at[pl.ds(0, total - 1)]
     waiter(bulk, row_recv).wait()
     gram_row = jnp.sum(gath[...], axis=0)
     weights = pcgrad_weights(gram_row, order_ref, groups)
 
-    @pl.loop(0, tiles)
+    @pl.loop(0, tiles, unroll=True)
     def _(tile):
         at = pl.ds(pl.multiple_of(tile * LANES, LANES), LANES)
         mixed = weights[0:1] * every[0, :, at].astype(jnp.float32)
@@ -363,7 +372,10 @@
                     waiter(block(task, index), fwd_send.at[task, index]).wait()
 
 
-def expand(acts_t, combined, weights_row, update_hbm, weights_ref, buffer, sems):
+def expand(acts_t, combined, weights_row, update_hbm, weights_hbm, buffer, few, sems, few_sem):
+    few[...] = weights_row[0, : few.shape[0]]
+    small = pltpu.make_async_copy(few, weights_hbm, few_sem)
+    small.start()
     rows = acts_t.shape[0]
     step = LANES if rows % LANES == 0 else rows
     copies = []
@@ -375,9 +387,9 @@
         copy = pltpu.make_async_copy(buffer.at[span], update_hbm.at[span], sems.at[n])
         copy.start()
         copies.append(copy)
-    weights_ref[...] = weights_row[0, : weights_ref.shape[0]]
     for copy in copies:
         copy.wait()
+    small.wait()
 
 
 def shards(acts, out_grads, order):
@@ -402,7 +414,7 @@
             pltpu.VMEM((1, LANES), jnp.float32),
         ),
         in_specs=[
-            pl.BlockSpec(memory_space=pltpu.SMEM),
+            pl.BlockSpec(memory_space=pltpu.HBM),
             pl.BlockSpec(memory_space=pltpu.HBM),
             pl.BlockSpec(memory_space=pltpu.HBM),
         ],
@@ -417,7 +429,7 @@
             pltpu.VMEM((16 if aligned else model, tokens), jnp.bfloat16),
             pltpu.VMEM((1, LANES), jnp.float32),
             pltpu.VMEM((total, 1, LANES), jnp.float32),
-            dma((2,)),
+            dma((3,)),
             dma((groups, groups)),
             dma((groups,)),
             dma((groups, groups)),
@@ -426,6 +438,7 @@
             dma,
             dma,
             pltpu.SemaphoreType.REGULAR((max(1, (others - 1).bit_length()),)),
+            pltpu.SMEM((groups,), jnp.int32),
         ],
         compiler_params=pltpu.CompilerParams(
             collective_id=0, has_side_effects=True, vmem_limit_bytes=VMEM_BYTES - kept
@@ -439,10 +452,12 @@
             jax.ShapeDtypeStruct((groups,), jnp.float32),
         ),
         in_specs=[vmem, vmem, vmem],
-        out_specs=(pl.BlockSpec(memory_space=pl.ANY), vmem),
+        out_specs=(pl.BlockSpec(memory_space=pl.ANY), pl.BlockSpec(memory_space=pl.ANY)),
         scratch_shapes=[
             pltpu.VMEM((part_rows, columns), jnp.float32),
+            pltpu.VMEM((groups,), jnp.float32),
             dma((pl.cdiv(part_rows, LANES),)),
+            dma,
         ],
         compiler_params=pltpu.CompilerParams(vmem_limit_bytes=24 * 2**20),
         name="expand",

time: 20.9 us -> 19.4 us (0.928)
  Pallas kernels: 20.1 us -> 18.6 us
    pallas_call x1, Pallas kernels: 17.2 us -> 16.1 us  [shards(): pl.pallas_call(functools.partial(mixer, groups, others), out_shape=(pltpu...]
    pallas_call x1, Pallas kernels: 2.94 us -> 2.45 us  [shards(): pl.pallas_call(expand, out_shape=(jax.ShapeDtypeStruct((part_rows, column...]
where the time goes in v4:
time: 19.4 us; the launch traced here: 19.2 us
  Pallas kernels  18.6 us (96%)
  between operations  0.64 us (3%)
    pallas_call x1, Pallas kernels, shards(): pl.pallas_call(functools.partial(mixer, groups, others), out_shape=(pltpu...  16.1 us
    pallas_call x1, Pallas kernels, shards(): pl.pallas_call(expand, out_shape=(jax.ShapeDtypeStruct((part_rows, column...  2.45 us

profile of v4, /device:TPU:0, one launch (start us, length us, event | category | flops | bytes accessed | tf_op | source)
XLA Modules:
  0.0 19.2 jit_solution(18106318128920885255)
XLA Ops:
  0.6 16.1 %mixer.1 = (bf16[128,1280]{1,0:T(8,128)(2,1)S(1)}, bf16[896,128]{1,0:T(8,128)(2,1)S(1)}, f32[1,128]{1,0:T(1,128)S(1)}) custom-call(s32[4]{0:T(128)} %order_hbm.1, bf16[128,3584]{1,0:T(8,128)(2,1)} %acts_hbm.1, bf16[1,128,1280]{2,1,0:T(8,128)(2,1)} %grads_hbm.1), custom_call_target="tpu_custom_call" | custom-call | tf_op jit(solution)/shard_map/mixer/pallas_call | solution.py:409
  16.8 2.4 %expand.1 = (f32[896,1280]{1,0:T(8,128)}, f32[4]{0:T(128)}) custom-call(bf16[896,128]{1,0:T(8,128)(2,1)S(1)} %get-tuple-element.5.acts_t, bf16[128,1280]{1,0:T(8,128)(2,1)S(1)} %get-tuple-element.6.combined, f32[1,128]{1,0:T(1,128)S(1)} %get-tuple-element.7.weights_row), custom_call_target="tpu_custom_call" | custom-call | tf_op jit(solution)/shard_map/expand/pallas_call | solution.py:448
